TPU v7x, 32 devices: a whole 2x2x4 slice. The times are simulated.
32 devices in a mesh: groups: 2 (over x), seq: 16 (over z, y, core).
Axes of the slice: x: 2, y: 2, z: 4, core: 2. Of those that a mesh axis runs over, the one named last changes fastest.
Arguments:
- queries: bfloat16 [8192, 4096], P(('groups', 'seq')), parts along dimension 0, may hold values from -6 to 6
- keys: bfloat16 [8192, 2048], P(('groups', 'seq')), parts along dimension 0, may hold values from -6 to 6
- values: bfloat16 [8192, 2048], P(('groups', 'seq')), parts along dimension 0, may hold values from -6 to 6
- doc_blocks: int32 [16], P('groups'), parts along dimension 0, may hold values from 1 to 8, 32 in all
Outputs:
- attended: bfloat16 [8192, 4096], P(('groups', 'seq')), parts along dimension 0
There are 2 independent parts, one for each index of `groups`. A program takes and returns all parts, laid end to end along the dimension named above; each array names one. Nothing has to cross between parts.
Inputs may be any that keep to these rules, and one draw needn't show every extreme that they name: `doc_blocks`: the lengths add up to 32; the longest document has exactly 8 units.
All inputs are finite; a program needn't handle non-finite values.
Results may differ from a plain program's by a relative error of at most 0.004.
Values may be sent and summed in bfloat16 or wider, within the bound.
No kernel may reach another device: no remote copies, remote signals or barrier semaphores. Data moves between devices by JAX's collectives and lax.ppermute only.
A program may use at most 64 MiB of HBM per device.

v0:
```python
import jax
import jax.numpy as jnp
from jax import lax
from jax.sharding import PartitionSpec as P

DH = 128
BLK = 128
score_scale = 144.0 ** (-0.5)


def from_partner(block, axis, bit):
    count = lax.axis_size(axis)
    route = []
    for low in range(count):
        high = low | 1 << bit
        if high != low and high < count:
            route += [(low, high), (high, low)]
    return lax.ppermute(block, axis, route)


def attend(
    query_heads, query_pos, all_keys, all_values, key_first, doc_blocks, query_block, key_block
):
    query_rows = query_heads.shape[0]
    key_here = query_heads.shape[1]
    ratio = query_heads.shape[2]
    lengths = doc_blocks * BLK
    doc_ends = jnp.cumsum(lengths)
    doc_starts = doc_ends - lengths
    doc_number = jnp.sum((query_pos[:, None] >= doc_ends[None, :]).astype(jnp.int32), axis=1)
    doc_ids = jnp.arange(doc_blocks.shape[0], dtype=jnp.int32)
    own_start = jnp.sum(
        jnp.where(doc_number[:, None] == doc_ids[None, :], doc_starts[None, :], 0), axis=1
    )

    def one_block(block_index):
        first_row = block_index * query_block
        query_tile = lax.dynamic_slice_in_dim(query_heads, first_row, query_block, 0)
        tile_pos = lax.dynamic_slice_in_dim(query_pos, first_row, query_block, 0)
        tile_start = lax.dynamic_slice_in_dim(own_start, first_row, query_block, 0)
        low_block = (tile_start[0] - key_first) // key_block
        high_block = (tile_pos[query_block - 1] - key_first) // key_block + 1
        state_shape = (key_here, ratio, query_block)
        start_state = (
            jnp.full(state_shape, -1e30, jnp.float32),
            jnp.zeros(state_shape, jnp.float32),
            jnp.zeros(state_shape + (DH,), jnp.float32),
        )

        def key_step(key_index, carried):
            run_max, run_total, run_sum = carried
            key_tile = lax.dynamic_slice_in_dim(all_keys, key_index * key_block, key_block, 0)
            value_tile = lax.dynamic_slice_in_dim(all_values, key_index * key_block, key_block, 0)
            scores = (
                jnp.einsum(
                    "qgsd,kgd->gsqk", query_tile, key_tile, preferred_element_type=jnp.float32
                )
                * score_scale
            )
            key_pos = key_first + key_index * key_block + jnp.arange(key_block, dtype=jnp.int32)
            visible = (key_pos[None, :] >= tile_start[:, None]) & (
                key_pos[None, :] <= tile_pos[:, None]
            )
            masked = jnp.where(visible, scores, -1e30)
            new_max = jnp.maximum(run_max, jnp.max(masked, axis=-1))
            rescale = jnp.exp(run_max - new_max)
            weights = jnp.where(visible, jnp.exp(scores - new_max[..., None]), 0.0)
            run_total = run_total * rescale + jnp.sum(weights, axis=-1)
            run_sum = run_sum * rescale[..., None] + jnp.einsum(
                "gsqk,kgd->gsqd",
                weights.astype(jnp.bfloat16),
                value_tile,
                preferred_element_type=jnp.float32,
            )
            return (new_max, run_total, run_sum)

        finished = lax.fori_loop(low_block, high_block, key_step, start_state)
        blended = finished[2] / finished[1][..., None]
        return (
            blended.transpose(2, 0, 1, 3)
            .reshape(query_block, key_here * ratio * DH)
            .astype(jnp.bfloat16)
        )

    blocks = lax.map(one_block, jnp.arange(query_rows // query_block, dtype=jnp.int32))
    return blocks.reshape(query_rows, key_here * ratio * DH)


def on_device(queries, keys, values, doc_blocks):
    axis_size = lax.axis_size("seq")
    my_index = lax.axis_index("seq")
    shard_rows = queries.shape[0]
    head_count = queries.shape[1] // DH
    key_count = keys.shape[1] // DH
    group_ratio = head_count // key_count
    total_rows = shard_rows * axis_size
    heads_here = max(1, head_count // axis_size)
    row_split = max(1, axis_size // head_count)
    head_groups = head_count // heads_here
    key_here = max(1, heads_here // group_ratio)
    key_groups = key_count // key_here
    copies = axis_size // key_groups
    part_rows = shard_rows // row_split
    query_width = heads_here * DH
    key_width = key_here * DH
    outgoing = queries.reshape(row_split, part_rows, head_groups, query_width).transpose(2, 0, 1, 3)
    outgoing = outgoing.reshape(axis_size, part_rows, query_width)
    got_queries = lax.all_to_all(outgoing, "seq", split_axis=0, concat_axis=0, tiled=True)
    piece_rows = shard_rows // copies
    stacked = jnp.stack((keys, values)).reshape(2, copies, piece_rows, key_groups, key_width)
    stacked = stacked.transpose(0, 3, 1, 2, 4).reshape(2, axis_size, piece_rows, key_width)
    got_pairs = lax.all_to_all(stacked, "seq", split_axis=1, concat_axis=1, tiled=True)
    gathered = got_pairs.reshape(2, axis_size, 1, piece_rows, key_width)
    for bit_number in range(copies.bit_length() - 1):
        partner = from_partner(gathered, "seq", bit_number)
        upper_half = my_index // 2**bit_number % 2 == 1
        gathered = jnp.where(
            upper_half,
            jnp.concatenate((partner, gathered), axis=2),
            jnp.concatenate((gathered, partner), axis=2),
        )
    pairs_flat = gathered.reshape(2, total_rows, key_here, DH)
    all_keys = pairs_flat[0]
    all_values = pairs_flat[1]
    query_rows = total_rows // row_split
    row_ids = jnp.arange(query_rows, dtype=jnp.int32)
    my_part = my_index % row_split
    query_pos = row_ids // part_rows * shard_rows + my_part * part_rows + row_ids % part_rows
    query_heads = got_queries.reshape(query_rows, key_here, heads_here // key_here, DH)
    result = attend(
        query_heads,
        query_pos,
        all_keys,
        all_values,
        0,
        doc_blocks,
        min(512, query_rows),
        min(512, total_rows),
    )
    result_parts = result.reshape(axis_size, part_rows, query_width)
    returned = lax.all_to_all(result_parts, "seq", split_axis=0, concat_axis=0, tiled=True)
    returned = returned.reshape(head_groups, row_split, part_rows, query_width).transpose(
        1, 2, 0, 3
    )
    return returned.reshape(shard_rows, head_count * DH)


def solution(mesh):
    in_specs = (
        P(("groups", "seq"), None),
        P(("groups", "seq"), None),
        P(("groups", "seq"), None),
        P("groups"),
    )
    out_specs = P(("groups", "seq"), None)
    return jax.shard_map(
        on_device, mesh=mesh, in_specs=in_specs, out_specs=out_specs, check_vma=False
    )
```

profile of v0, /device:TPU:11, one launch (start us, length us, event | category | flops | bytes accessed | tf_op | source)
XLA Modules:
  0.0 290.4 jit_solution(64911163191725977)
XLA Ops:
  0.0 4.1 %copy.34 = bf16[256,4096]{0,1:T(8,128)(2,1)} copy(bf16[256,4096]{1,0:T(8,128)(2,1)} %param.8) | data formatting | bytes 4194304 | tf_op args[0]
  4.1 6.6 %all-to-all-start = ((bf16[16,256,256]{1,2,0:T(8,128)(2,1)}), bf16[16,256,256]{1,2,0:T(8,128)(2,1)S(1)}, u32[]{:S(2)}, u32[]{:S(2)}) async-start(bf16[16,256,256]{1,2,0:T(8,128)(2,1)} %bitcast.116), calls=%async_computation | async-start | bytes 4194304 | tf_op jit(solution)/shard_map/all_to_all | solution.py:108
  10.6 1.5 copy.36
  12.1 2.3 copy.37
  14.4 2.8 maximum_bitcast_fusion
  17.2 4.0 %copy.38 = bf16[2,16,256,128]{3,2,0,1:T(8,128)(2,1)} copy(bf16[2,16,256,128]{2,3,1,0:T(8,128)(2,1)} %maximum_bitcast_fusion) | data formatting | bytes 4194304 | tf_op jit(solution)/shard_map/reshape | solution.py:111
  21.1 35.6 %all-to-all-done = bf16[16,256,256]{1,2,0:T(8,128)(2,1)S(1)} async-done(((bf16[16,256,256]{1,2,0:T(8,128)(2,1)}), bf16[16,256,256]{1,2,0:T(8,128)(2,1)S(1)}, u32[]{:S(2)}, u32[]{:S(2)}) %all-to-all-start) | async-done | bytes 2097184 | tf_op jit(solution)/shard_map/all_to_all | solution.py:108
  56.7 6.1 %all-to-all-start.1 = ((bf16[2,16,256,128]{3,2,0,1:T(8,128)(2,1)}), bf16[2,16,256,128]{3,2,0,1:T(8,128)(2,1)}, u32[]{:S(2)}, u32[]{:S(2)}) async-start(bf16[2,16,256,128]{3,2,0,1:T(8,128)(2,1)} %copy.38), calls=%async_computation.1 | async-start | bytes 4194304 | tf_op jit(solution)/shard_map/all_to_all | solution.py:112
  63.3 2.5 copy.35
  65.8 4.2 %reshape.133 = bf16[4096,1,2,128]{0,3,2,1:T(8,128)(2,1)} reshape(bf16[16,256,256]{1,0,2:T(8,128)(2,1)} %copy.35) | data formatting | bytes 4194304 | tf_op jit(solution)/shard_map/reshape | solution.py:129
  70.0 39.0 %all-to-all-done.1 = bf16[2,16,256,128]{3,2,0,1:T(8,128)(2,1)} async-done(((bf16[2,16,256,128]{3,2,0,1:T(8,128)(2,1)}), bf16[2,16,256,128]{3,2,0,1:T(8,128)(2,1)}, u32[]{:S(2)}, u32[]{:S(2)}) %all-to-all-start.1) | async-done | bytes 2097184 | tf_op jit(solution)/shard_map/all_to_all | solution.py:112
  109.0 1.7 fusion.33
  110.8 119.2 %while.44 = (s32[]{:T(128)}, bf16[8,512,256]{2,1,0:T(8,128)(2,1)}, s32[8]{0:T(128)S(1)}, s32[4096]{0:T(1024)S(1)}, s32[4096]{0:T(1024)S(1)}, /*index=5*/bf16[409...) while((s32[]{:T(128)}, bf16[8,512,256]{2,1,0:T(8,128)(2,1)}, ...), condition=%wide.region_8.9_spmd, body=%wide.region_3.8_spmd.sunk | while | flops 275516960 | bytes 12940678 | solution.py:85
  110.8 0.6 dynamic_slice.53
  112.1 0.6 slice.31
  118.2 1.0 constant_dynamic-slice_fusion.2
  119.5 2.3 while.45
  120.4 0.8 fusion.47
  122.4 0.7 constant_dynamic-update-slice_fusion.2
  130.6 1.0 constant_dynamic-slice_fusion.2
  131.8 4.5 %while.45 = (s32[]{:T(128)}, f32[1,2,512]{2,1,0:T(2,128)S(1)}, f32[1,2,512]{2,1,0:T(2,128)S(1)}, f32[1,2,512,128]{3,2,1,0:T(8,128)S(1)}, s32[]{:T(128)}, /*index...) while((s32[]{:T(128)}, f32[1,2,512]{2,1,0:T(2,128)S(1)}, ...), condition=%wide.region_7.7_spmd, body=%wide.region_4.6_spmd.sunk | while | flops 275254784 | bytes 8986815 | solution.py:77
  132.7 0.8 fusion.47
  135.0 0.8 fusion.47
  137.0 0.7 constant_dynamic-update-slice_fusion.2
  139.1 0.6 slice.31
  145.2 1.0 constant_dynamic-slice_fusion.2
  146.4 4.5 %while.45 = (s32[]{:T(128)}, f32[1,2,512]{2,1,0:T(2,128)S(1)}, f32[1,2,512]{2,1,0:T(2,128)S(1)}, f32[1,2,512,128]{3,2,1,0:T(8,128)S(1)}, s32[]{:T(128)}, /*index...) while((s32[]{:T(128)}, f32[1,2,512]{2,1,0:T(2,128)S(1)}, ...), condition=%wide.region_7.7_spmd, body=%wide.region_4.6_spmd.sunk | while | flops 275254784 | bytes 8986815 | solution.py:77
  147.3 0.8 fusion.47
  149.6 0.8 fusion.47
  151.7 0.7 constant_dynamic-update-slice_fusion.2
  153.7 0.6 slice.31
  159.8 1.0 constant_dynamic-slice_fusion.2
  161.0 6.8 %while.45 = (s32[]{:T(128)}, f32[1,2,512]{2,1,0:T(2,128)S(1)}, f32[1,2,512]{2,1,0:T(2,128)S(1)}, f32[1,2,512,128]{3,2,1,0:T(8,128)S(1)}, s32[]{:T(128)}, /*index...) while((s32[]{:T(128)}, f32[1,2,512]{2,1,0:T(2,128)S(1)}, ...), condition=%wide.region_7.7_spmd, body=%wide.region_4.6_spmd.sunk | while | flops 275254784 | bytes 8986815 | solution.py:77
  161.9 0.8 fusion.47
  164.2 0.8 fusion.47
  166.5 0.8 fusion.47
  168.5 0.7 constant_dynamic-update-slice_fusion.2
  170.6 0.6 slice.31
  176.7 1.0 constant_dynamic-slice_fusion.2
  177.9 4.5 %while.45 = (s32[]{:T(128)}, f32[1,2,512]{2,1,0:T(2,128)S(1)}, f32[1,2,512]{2,1,0:T(2,128)S(1)}, f32[1,2,512,128]{3,2,1,0:T(8,128)S(1)}, s32[]{:T(128)}, /*index...) while((s32[]{:T(128)}, f32[1,2,512]{2,1,0:T(2,128)S(1)}, ...), condition=%wide.region_7.7_spmd, body=%wide.region_4.6_spmd.sunk | while | flops 275254784 | bytes 8986815 | solution.py:77
  178.8 0.8 fusion.47
  181.1 0.8 fusion.47
  183.2 0.7 constant_dynamic-update-slice_fusion.2
  185.2 0.6 slice.31
  191.3 1.0 constant_dynamic-slice_fusion.2
  192.6 4.5 %while.45 = (s32[]{:T(128)}, f32[1,2,512]{2,1,0:T(2,128)S(1)}, f32[1,2,512]{2,1,0:T(2,128)S(1)}, f32[1,2,512,128]{3,2,1,0:T(8,128)S(1)}, s32[]{:T(128)}, /*index...) while((s32[]{:T(128)}, f32[1,2,512]{2,1,0:T(2,128)S(1)}, ...), condition=%wide.region_7.7_spmd, body=%wide.region_4.6_spmd.sunk | while | flops 275254784 | bytes 8986815 | solution.py:77
  193.4 0.8 fusion.47
  195.7 0.8 fusion.47
  197.8 0.7 constant_dynamic-update-slice_fusion.2
  206.0 1.0 constant_dynamic-slice_fusion.2
  207.2 4.5 %while.45 = (s32[]{:T(128)}, f32[1,2,512]{2,1,0:T(2,128)S(1)}, f32[1,2,512]{2,1,0:T(2,128)S(1)}, f32[1,2,512,128]{3,2,1,0:T(8,128)S(1)}, s32[]{:T(128)}, /*index...) while((s32[]{:T(128)}, f32[1,2,512]{2,1,0:T(2,128)S(1)}, ...), condition=%wide.region_7.7_spmd, body=%wide.region_4.6_spmd.sunk | while | flops 275254784 | bytes 8986815 | solution.py:77
  208.1 0.8 fusion.47
  210.3 0.8 fusion.47
  212.4 0.7 constant_dynamic-update-slice_fusion.2
  214.4 0.6 slice.31
  220.6 1.0 constant_dynamic-slice_fusion.2
  221.8 6.8 %while.45 = (s32[]{:T(128)}, f32[1,2,512]{2,1,0:T(2,128)S(1)}, f32[1,2,512]{2,1,0:T(2,128)S(1)}, f32[1,2,512,128]{3,2,1,0:T(8,128)S(1)}, s32[]{:T(128)}, /*index...) while((s32[]{:T(128)}, f32[1,2,512]{2,1,0:T(2,128)S(1)}, ...), condition=%wide.region_7.7_spmd, body=%wide.region_4.6_spmd.sunk | while | flops 275254784 | bytes 8986815 | solution.py:77
  222.7 0.8 fusion.47
  224.9 0.8 fusion.47
  227.2 0.8 fusion.47
  229.3 0.7 constant_dynamic-update-slice_fusion.2
  230.0 53.9 %all_to_all.15 = bf16[16,256,256]{2,1,0:T(8,128)(2,1)S(1)} all-to-all(bf16[16,256,256]{2,1,0:T(8,128)(2,1)} %bitcast.121), channel_id=1, replica_groups=mesh['groups'=2,'seq'=16] {'seq'}, dimensions={0} | all-to-all | bytes 4194304 | tf_op jit(solution)/shard_map/all_to_all | solution.py:141
  283.9 2.4 copy.40
  286.3 4.1 %copy.41 = bf16[256,4096]{1,0:T(8,128)(2,1)} copy(bf16[256,4096]{0,1:T(8,128)(2,1)} %bitcast.117) | data formatting | bytes 4194304 | tf_op jit(solution)/shard_map/reshape | solution.py:145
  (218 shorter events, 41.3 us)
Async XLA Ops:
  4.1 52.7 %all-to-all-start = ((bf16[16,256,256]{1,2,0:T(8,128)(2,1)}), bf16[16,256,256]{1,2,0:T(8,128)(2,1)S(1)}, u32[]{:S(2)}, u32[]{:S(2)}) async-start(bf16[16,256,256]{1,2,0:T(8,128)(2,1)} %bitcast.116), calls=%async_computation | async-start | bytes 4194304 | tf_op jit(solution)/shard_map/all_to_all | solution.py:108
  21.1 41.7 %copy-start = (s32[8]{0:T(128)S(1)}, s32[8]{0:T(128)}, u32[]{:S(2)}) copy-start(s32[8]{0:T(128)} %param.11) | copy-start | bytes 100
  56.7 52.3 %all-to-all-start.1 = ((bf16[2,16,256,128]{3,2,0,1:T(8,128)(2,1)}), bf16[2,16,256,128]{3,2,0,1:T(8,128)(2,1)}, u32[]{:S(2)}, u32[]{:S(2)}) async-start(bf16[2,16,256,128]{3,2,0,1:T(8,128)(2,1)} %copy.38), calls=%async_computation.1 | async-start | bytes 4194304 | tf_op jit(solution)/shard_map/all_to_all | solution.py:112
where the time goes:
time: 292 us; the launch traced here: 290 us
  waiting for transfers between devices  74.6 us (26%)
  local copies, waits for them, and re-layouts  60.7 us (21%)
  blocking collectives  53.9 us (18%)
  loops' own time  46.3 us (16%)
  matrix products  23.7 us (8%)
  other arithmetic  18.4 us (6%)
  starting transfers between devices  12.7 us (4%)
    all_to_all x1, blocking collectives, on_device(): lax.all_to_all(result_parts, 'seq', split_axis=0, concat_axis=0, tiled=True)  53.9 us
    another operation x1, loops' own time, attend(): lax.map(one_block, jnp.arange(query_rows // query_block, dtype=jnp.int32))  45 us
    all_to_all x1, waiting for transfers between devices, on_device(): lax.all_to_all(stacked, 'seq', split_axis=1, concat_axis=1, tiled=True)  39 us
    all_to_all x1, waiting for transfers between devices, on_device(): lax.all_to_all(outgoing, 'seq', split_axis=0, concat_axis=0, tiled=True)  35.6 us
    dot_general x17, matrix products, key_step(): jnp.einsum('gsqk,kgd->gsqd', weights.astype(jnp.bfloat16), value_tile, pr...  14.3 us
    dot_general x17, matrix products, key_step(): jnp.einsum('qgsd,kgd->gsqk', query_tile, key_tile, preferred_element_type...  9.37 us
    dynamic_slice x16, local copies, waits for them, and re-layouts, one_block(): lax.dynamic_slice_in_dim(query_heads, first_row, query_block, 0)  9.15 us
    reduce_sum x17, other arithmetic, key_step(): run_total = run_total * rescale + jnp.sum(weights, axis=-1)  8.43 us
  transfers between devices with their start and end apart: 2, of which 2 were waited for; matrix products, arithmetic and copies ran while one was open for 6% of the time, Pallas kernels for 0%

commit v1 on v0

--- a/solution.py
+++ b/solution.py
@@ -109,7 +109,10 @@
     piece_rows = shard_rows // copies
     stacked = jnp.stack((keys, values)).reshape(2, copies, piece_rows, key_groups, key_width)
     stacked = stacked.transpose(0, 3, 1, 2, 4).reshape(2, axis_size, piece_rows, key_width)
-    got_pairs = lax.all_to_all(stacked, "seq", split_axis=1, concat_axis=1, tiled=True)
+    got_pairs = jnp.concatenate(
+        lax.all_to_all(jnp.stack(jnp.split(stacked, lax.axis_size("seq"), axis=1)), "seq", 0, 0),
+        axis=1,
+    )
     gathered = got_pairs.reshape(2, axis_size, 1, piece_rows, key_width)
     for bit_number in range(copies.bit_length() - 1):
         partner = from_partner(gathered, "seq", bit_number)

time: 292 us -> 312 us (1.068)
  matrix products: 23.7 us -> 39.1 us
  waiting for transfers between devices: 74.6 us -> 86.6 us
  local copies, waits for them, and re-layouts: 60.7 us -> 55.4 us
    dot_general x17, matrix products: 14.3 us -> 29.7 us  [key_step(): jnp.einsum('gsqk,kgd->gsqd', weights.astype(jnp.bfloat16), value_tile, pr...]
    all_to_all x1, waiting for transfers between devices: 35.6 us -> 44.6 us  [on_device(): lax.all_to_all(outgoing, 'seq', split_axis=0, concat_axis=0, tiled=True)]
    reshape x1 -> x0, local copies, waits for them, and re-layouts: 3.95 us -> none  [on_device(): stacked.transpose(0, 3, 1, 2, 4)]
    unnamed x5 -> x22, local copies, waits for them, and re-layouts: 7.83 us -> 6.34 us
  transfers between devices with their start and end apart: 2 -> 2, of which waited for: 2 -> 2; matrix products, arithmetic and copies ran while one was open for 6% -> 2% of each run, Pallas kernels for 0% -> 0%
where the time goes in v1:
time: 312 us; the launch traced here: 310 us
  waiting for transfers between devices  86.6 us (28%)
  local copies, waits for them, and re-layouts  55.4 us (18%)
  blocking collectives  53.9 us (17%)
  loops' own time  46.3 us (15%)
  matrix products  39.1 us (13%)
  other arithmetic  15.9 us (5%)
  starting transfers between devices  12.8 us (4%)
    all_to_all x1, blocking collectives, on_device(): lax.all_to_all(result_parts, 'seq', split_axis=0, concat_axis=0, tiled=True)  53.9 us
    another operation x1, loops' own time, attend(): lax.map(one_block, jnp.arange(query_rows // query_block, dtype=jnp.int32))  45 us
    all_to_all x1, waiting for transfers between devices, on_device(): lax.all_to_all(outgoing, 'seq', split_axis=0, concat_axis=0, tiled=True)  44.6 us
    all_to_all x1, waiting for transfers between devices, on_device(): lax.all_to_all(jnp.stack(jnp.split(stacked, lax.axis_size('seq'), axis=1)...  42 us
    dot_general x17, matrix products, key_step(): jnp.einsum('gsqk,kgd->gsqd', weights.astype(jnp.bfloat16), value_tile, pr...  29.7 us
    dot_general x17, matrix products, key_step(): jnp.einsum('qgsd,kgd->gsqk', query_tile, key_tile, preferred_element_type...  9.38 us
    dynamic_slice x16, local copies, waits for them, and re-layouts, one_block(): lax.dynamic_slice_in_dim(query_heads, first_row, query_block, 0)  9.15 us
    reduce_sum x17, other arithmetic, key_step(): run_total = run_total * rescale + jnp.sum(weights, axis=-1)  8.43 us
  transfers between devices with their start and end apart: 2, of which 2 were waited for; matrix products, arithmetic and copies ran while one was open for 2% of the time, Pallas kernels for 0%

profile of v1, /device:TPU:11, one launch (start us, length us, event | category | flops | bytes accessed | tf_op | source)
XLA Modules:
  0.0 310.2 jit_solution(16234062451891943363)
XLA Ops:
  0.0 1.6 copy.96
  2.6 2.4 copy.113
  5.0 6.6 %all-to-all-start.1 = ((bf16[16,2,1,256,128]{4,3,2,1,0:T(8,128)(2,1)}), bf16[16,2,1,256,128]{4,3,2,1,0:T(8,128)(2,1)S(1)}, u32[]{:S(2)}, u32[]{:S(2)}) async-start(bf16[16,2,1,256,128]{4,3,2,1,0:T(8,128)(2,1)} %copy.113), calls=%async_computation.1 | async-start | bytes 4194304 | tf_op jit(solution)/shard_map/all_to_all | solution.py:113
  11.6 4.1 %copy.94 = bf16[256,4096]{0,1:T(8,128)(2,1)} copy(bf16[256,4096]{1,0:T(8,128)(2,1)} %param.8) | data formatting | bytes 4194304 | tf_op args[0]
  15.7 42.0 %all-to-all-done.1 = bf16[16,2,1,256,128]{4,3,2,1,0:T(8,128)(2,1)S(1)} async-done(((bf16[16,2,1,256,128]{4,3,2,1,0:T(8,128)(2,1)}), bf16[16,2,1,256,128]{4,3,2,1,0:T(8,128)(2,1)S(1)}, u32[]{:S(2)}, u32[]{:S(2)}) %all-to-all-start.1) | async-done | bytes 2097184 | tf_op jit(solution)/shard_map/all_to_all | solution.py:113
  57.7 6.2 %all-to-all-start = ((bf16[16,256,256]{1,2,0:T(8,128)(2,1)}), bf16[16,256,256]{1,2,0:T(8,128)(2,1)}, u32[]{:S(2)}, u32[]{:S(2)}) async-start(bf16[16,256,256]{1,2,0:T(8,128)(2,1)} %bitcast.212), calls=%async_computation | async-start | bytes 4194304 | tf_op jit(solution)/shard_map/all_to_all | solution.py:108
  64.4 1.1 fusion.49
  65.5 44.6 %all-to-all-done = bf16[16,256,256]{1,2,0:T(8,128)(2,1)} async-done(((bf16[16,256,256]{1,2,0:T(8,128)(2,1)}), bf16[16,256,256]{1,2,0:T(8,128)(2,1)}, u32[]{:S(2)}, u32[]{:S(2)}) %all-to-all-start) | async-done | bytes 2097184 | tf_op jit(solution)/shard_map/all_to_all | solution.py:108
  110.1 2.8 copy.95
  112.9 2.4 reshape.136
  115.2 134.6 %while.44 = (s32[]{:T(128)}, bf16[8,512,256]{2,1,0:T(8,128)(2,1)}, s32[8]{0:T(128)S(1)}, s32[4096]{0:T(1024)S(1)}, s32[4096]{0:T(1024)S(1)}, /*index=5*/bf16[409...) while((s32[]{:T(128)}, bf16[8,512,256]{2,1,0:T(8,128)(2,1)}, ...), condition=%wide.region_8.9_spmd, body=%wide.region_3.8_spmd.sunk | while | flops 275516960 | bytes 12940678 | solution.py:85
  115.2 0.6 dynamic_slice.53
  116.5 0.6 slice.31
  122.7 1.0 constant_dynamic-slice_fusion.2
  123.9 3.2 %while.45 = (s32[]{:T(128)}, f32[1,2,512]{2,1,0:T(2,128)S(1)}, f32[1,2,512]{2,1,0:T(2,128)S(1)}, f32[1,2,512,128]{3,2,1,0:T(8,128)S(1)}, s32[]{:T(128)}, /*index...) while((s32[]{:T(128)}, f32[1,2,512]{2,1,0:T(2,128)S(1)}, ...), condition=%wide.region_7.7_spmd, body=%wide.region_4.6_spmd.sunk | while | flops 275254784 | bytes 8986815 | solution.py:77
  124.8 1.7 fusion.63
  127.8 0.7 constant_dynamic-update-slice_fusion.2
  129.8 0.6 slice.31
  136.0 1.0 constant_dynamic-slice_fusion.2
  137.2 6.4 %while.45 = (s32[]{:T(128)}, f32[1,2,512]{2,1,0:T(2,128)S(1)}, f32[1,2,512]{2,1,0:T(2,128)S(1)}, f32[1,2,512,128]{3,2,1,0:T(8,128)S(1)}, s32[]{:T(128)}, /*index...) while((s32[]{:T(128)}, f32[1,2,512]{2,1,0:T(2,128)S(1)}, ...), condition=%wide.region_7.7_spmd, body=%wide.region_4.6_spmd.sunk | while | flops 275254784 | bytes 8986815 | solution.py:77
  138.1 1.7 fusion.63
  141.2 1.7 fusion.63
  144.2 0.7 constant_dynamic-update-slice_fusion.2
  146.2 0.6 slice.31
  152.4 1.0 constant_dynamic-slice_fusion.2
  153.6 6.4 %while.45 = (s32[]{:T(128)}, f32[1,2,512]{2,1,0:T(2,128)S(1)}, f32[1,2,512]{2,1,0:T(2,128)S(1)}, f32[1,2,512,128]{3,2,1,0:T(8,128)S(1)}, s32[]{:T(128)}, /*index...) while((s32[]{:T(128)}, f32[1,2,512]{2,1,0:T(2,128)S(1)}, ...), condition=%wide.region_7.7_spmd, body=%wide.region_4.6_spmd.sunk | while | flops 275254784 | bytes 8986815 | solution.py:77
  154.5 1.7 fusion.63
  157.7 1.7 fusion.63
  160.6 0.7 constant_dynamic-update-slice_fusion.2
  162.7 0.6 slice.31
  168.8 1.0 constant_dynamic-slice_fusion.2
  170.0 9.5 %while.45 = (s32[]{:T(128)}, f32[1,2,512]{2,1,0:T(2,128)S(1)}, f32[1,2,512]{2,1,0:T(2,128)S(1)}, f32[1,2,512,128]{3,2,1,0:T(8,128)S(1)}, s32[]{:T(128)}, /*index...) while((s32[]{:T(128)}, f32[1,2,512]{2,1,0:T(2,128)S(1)}, ...), condition=%wide.region_7.7_spmd, body=%wide.region_4.6_spmd.sunk | while | flops 275254784 | bytes 8986815 | solution.py:77
  170.9 1.7 fusion.63
  174.1 1.7 fusion.63
  177.3 1.7 fusion.63
  180.3 0.7 constant_dynamic-update-slice_fusion.2
  182.3 0.6 slice.31
  188.4 1.0 constant_dynamic-slice_fusion.2
  189.6 6.4 %while.45 = (s32[]{:T(128)}, f32[1,2,512]{2,1,0:T(2,128)S(1)}, f32[1,2,512]{2,1,0:T(2,128)S(1)}, f32[1,2,512,128]{3,2,1,0:T(8,128)S(1)}, s32[]{:T(128)}, /*index...) while((s32[]{:T(128)}, f32[1,2,512]{2,1,0:T(2,128)S(1)}, ...), condition=%wide.region_7.7_spmd, body=%wide.region_4.6_spmd.sunk | while | flops 275254784 | bytes 8986815 | solution.py:77
  190.5 1.7 fusion.63
  193.7 1.7 fusion.63
  196.7 0.7 constant_dynamic-update-slice_fusion.2
  198.7 0.6 slice.31
  204.9 1.0 constant_dynamic-slice_fusion.2
  206.1 6.4 %while.45 = (s32[]{:T(128)}, f32[1,2,512]{2,1,0:T(2,128)S(1)}, f32[1,2,512]{2,1,0:T(2,128)S(1)}, f32[1,2,512,128]{3,2,1,0:T(8,128)S(1)}, s32[]{:T(128)}, /*index...) while((s32[]{:T(128)}, f32[1,2,512]{2,1,0:T(2,128)S(1)}, ...), condition=%wide.region_7.7_spmd, body=%wide.region_4.6_spmd.sunk | while | flops 275254784 | bytes 8986815 | solution.py:77
  207.0 1.7 fusion.63
  210.1 1.7 fusion.63
  213.1 0.7 constant_dynamic-update-slice_fusion.2
  215.1 0.6 slice.31
  221.3 1.0 constant_dynamic-slice_fusion.2
  222.5 6.4 %while.45 = (s32[]{:T(128)}, f32[1,2,512]{2,1,0:T(2,128)S(1)}, f32[1,2,512]{2,1,0:T(2,128)S(1)}, f32[1,2,512,128]{3,2,1,0:T(8,128)S(1)}, s32[]{:T(128)}, /*index...) while((s32[]{:T(128)}, f32[1,2,512]{2,1,0:T(2,128)S(1)}, ...), condition=%wide.region_7.7_spmd, body=%wide.region_4.6_spmd.sunk | while | flops 275254784 | bytes 8986815 | solution.py:77
  223.4 1.7 fusion.63
  226.6 1.7 fusion.63
  229.5 0.7 constant_dynamic-update-slice_fusion.2
  231.6 0.6 slice.31
  237.7 1.0 constant_dynamic-slice_fusion.2
  238.9 9.5 %while.45 = (s32[]{:T(128)}, f32[1,2,512]{2,1,0:T(2,128)S(1)}, f32[1,2,512]{2,1,0:T(2,128)S(1)}, f32[1,2,512,128]{3,2,1,0:T(8,128)S(1)}, s32[]{:T(128)}, /*index...) while((s32[]{:T(128)}, f32[1,2,512]{2,1,0:T(2,128)S(1)}, ...), condition=%wide.region_7.7_spmd, body=%wide.region_4.6_spmd.sunk | while | flops 275254784 | bytes 8986815 | solution.py:77
  239.8 1.7 fusion.63
  243.0 1.7 fusion.63
  246.2 1.7 fusion.63
  249.1 0.7 constant_dynamic-update-slice_fusion.2
  249.9 53.9 %all_to_all.15 = bf16[16,256,256]{2,1,0:T(8,128)(2,1)S(1)} all-to-all(bf16[16,256,256]{2,1,0:T(8,128)(2,1)} %bitcast.217), channel_id=1, replica_groups=mesh['groups'=2,'seq'=16] {'seq'}, dimensions={0} | all-to-all | bytes 4194304 | tf_op jit(solution)/shard_map/all_to_all | solution.py:144
  303.8 2.4 copy.115
  306.2 4.1 %copy.116 = bf16[256,4096]{1,0:T(8,128)(2,1)} copy(bf16[256,4096]{0,1:T(8,128)(2,1)} %bitcast.213) | data formatting | bytes 4194304 | tf_op jit(solution)/shard_map/reshape | solution.py:148
  (236 shorter events, 41.0 us)
Async XLA Ops:
  0.0 1.6 copy-start
  5.0 52.7 %all-to-all-start.1 = ((bf16[16,2,1,256,128]{4,3,2,1,0:T(8,128)(2,1)}), bf16[16,2,1,256,128]{4,3,2,1,0:T(8,128)(2,1)S(1)}, u32[]{:S(2)}, u32[]{:S(2)}) async-start(bf16[16,2,1,256,128]{4,3,2,1,0:T(8,128)(2,1)} %copy.113), calls=%async_computation.1 | async-start | bytes 4194304 | tf_op jit(solution)/shard_map/all_to_all | solution.py:113
  57.7 6.3 %copy-start.1 = (s32[8]{0:T(128)S(1)}, s32[8]{0:T(128)}, u32[]{:S(2)}) copy-start(s32[8]{0:T(128)} %param.11) | copy-start | bytes 100
  57.7 52.4 %all-to-all-start = ((bf16[16,256,256]{1,2,0:T(8,128)(2,1)}), bf16[16,256,256]{1,2,0:T(8,128)(2,1)}, u32[]{:S(2)}, u32[]{:S(2)}) async-start(bf16[16,256,256]{1,2,0:T(8,128)(2,1)} %bitcast.212), calls=%async_computation | async-start | bytes 4194304 | tf_op jit(solution)/shard_map/all_to_all | solution.py:108
